TPU v7x, 32 devices: a whole 2x2x4 slice. The times are simulated.
32 devices in a mesh: cfg: 2 (over y), expert: 4 (over z), ffn: 4 (over x, core).
Axes of the slice: x: 2, y: 2, z: 4, core: 2. Of those that a mesh axis runs over, the one named last changes fastest.
Arguments:
- tokens: bfloat16 [2048, 2048], P(('cfg', 'expert'), 'ffn'), parts along dimension 0, may hold values from -6 to 6
- chosen: int32 [8, 512], P(('cfg', 'expert')), parts along dimension 0, may hold values from 0 to 1023, as said below
- gates: float32 [8, 512], P(('cfg', 'expert')), parts along dimension 0, may hold values from 0.1 to 1
- capacity: int32 [2], P('cfg'), parts along dimension 0, may hold values from 256 to 512
- w_gate: bfloat16 [4, 2048, 1024], P('expert', None, 'ffn'), may hold values from -0.125 to 0.125
- w_up: bfloat16 [4, 2048, 1024], P('expert', None, 'ffn'), may hold values from -0.125 to 0.125
- w_down: bfloat16 [4, 1024, 2048], P('expert', 'ffn'), may hold values from -0.1875 to 0.1875
Outputs:
- mixed: bfloat16 [2048, 2048], P(('cfg', 'expert'), 'ffn'), parts along dimension 0
There are 2 independent parts, one for each index of `cfg`. A program takes and returns all parts, laid end to end along the dimension named above; an argument that names none is the same for every part. Nothing has to cross between parts.
Inputs may be any that keep to these rules, and one draw needn't show every extreme that they name: `chosen`: each row lists 512 different tokens; at most 256 of one row's tokens lie in one aligned block of 256 tokens, and every row has exactly 256 in some block.
All inputs are finite; a program needn't handle non-finite values.
Results may differ from a plain program's by a relative error of at most 0.013.
Values may be sent and summed in bfloat16 or wider, within the bound.
A program may use at most 64 MiB of HBM per device.

v0:
```python
import jax
import jax.numpy as jnp
from jax import lax
from jax.sharding import PartitionSpec as P


def shards(tokens, chosen, gates, capacity, w_gate, w_up, w_down):
    experts_n = lax.axis_size("expert")
    tok_dev = tokens.shape[0]
    picked_ids = chosen[0]
    listed = picked_ids.shape[0]
    slot_depth = 2 * listed // experts_n
    positions = jnp.arange(listed, dtype=jnp.int32)
    alive_mask = positions < capacity[0]
    weights = jnp.where(alive_mask, gates[0], jnp.zeros_like(gates[0]))
    source = picked_ids // tok_dev
    offset = picked_ids - source * tok_dev
    member = (source[:, None] == jnp.arange(experts_n, dtype=jnp.int32)[None, :]).astype(jnp.int32)
    before = jnp.cumsum(member, axis=0) - member
    rank_in = jnp.sum(before * member, axis=1)
    slot_of = source * slot_depth + rank_in
    wanted = jnp.where(alive_mask, offset, -1)
    request = jnp.full((experts_n * slot_depth,), -1, jnp.int32).at[slot_of].set(wanted)
    requested = lax.all_to_all(
        request.reshape(experts_n, slot_depth), "expert", split_axis=0, concat_axis=0, tiled=True
    ).reshape(-1)
    usable = requested >= 0
    safe_idx = jnp.maximum(requested, 0)
    gate_cols = w_gate[0]
    up_cols = w_up[0]
    down_rows = w_down[0]
    row_block = jnp.where(
        usable[:, None], jnp.take(tokens, safe_idx, axis=0), jnp.zeros((), jnp.bfloat16)
    )
    slots = lax.all_to_all(
        row_block.reshape(experts_n, slot_depth, -1),
        "expert",
        split_axis=0,
        concat_axis=0,
        tiled=True,
    )
    picked = jnp.take(slots.reshape(experts_n * slot_depth, -1), slot_of, axis=0)
    portion = lax.all_gather(picked, "ffn", axis=1, tiled=True)
    gate_next = jnp.dot(portion, gate_cols, preferred_element_type=jnp.float32)
    up_next = jnp.dot(portion, up_cols, preferred_element_type=jnp.float32)
    hidden = (jax.nn.silu(gate_next) * up_next).astype(jnp.bfloat16)
    partial_value = jnp.dot(hidden, down_rows, preferred_element_type=jnp.float32)
    summed = lax.psum_scatter(
        partial_value.astype(jnp.bfloat16), "ffn", scatter_dimension=1, tiled=True
    ).astype(jnp.float32)
    contribution = (weights[:, None] * summed).astype(jnp.bfloat16)
    returned_slots = (
        jnp.zeros((experts_n * slot_depth, contribution.shape[1]), jnp.bfloat16)
        .at[slot_of]
        .set(contribution)
    )
    returned = lax.all_to_all(
        returned_slots.reshape(experts_n, slot_depth, -1),
        "expert",
        split_axis=0,
        concat_axis=0,
        tiled=True,
    )
    returned = returned.reshape(experts_n * slot_depth, -1)
    placement_map = (requested[None, :] == jnp.arange(tok_dev, dtype=jnp.int32)[:, None]).astype(
        jnp.bfloat16
    )
    mixed = jnp.dot(placement_map, returned, preferred_element_type=jnp.float32)
    return mixed.astype(jnp.bfloat16)


def solution(mesh):
    in_specs = (
        P(("cfg", "expert"), "ffn"),
        P(("cfg", "expert"), None),
        P(("cfg", "expert"), None),
        P("cfg"),
        P("expert", None, "ffn"),
        P("expert", None, "ffn"),
        P("expert", "ffn", None),
    )
    out_specs = P(("cfg", "expert"), "ffn")
    return jax.shard_map(shards, mesh=mesh, in_specs=in_specs, out_specs=out_specs, check_vma=False)
```

profile of v0, /device:TPU:0, one launch (start us, length us, event | category | flops | bytes accessed | tf_op | source)
XLA Modules:
  0.0 165.5 jit_solution(15159481432973345093)
XLA Ops:
  6.5 0.0 copy-start
  7.3 0.7 add_select_fusion
  8.0 1.2 reduce-window.6
  9.2 0.2 slice_reduce_fusion
  9.4 0.2 reduce-window.9
  9.6 0.1 add_bitcast_fusion
  9.7 0.7 subtract_select_fusion
  10.4 0.7 compare_select_fusion
  11.1 2.4 %scatter_custom_fusion = s32[1024]{0:T(1024)S(1)} fusion(s32[512]{0:T(512)S(1)} %bitcast.71, s32[512]{0:T(512)S(1)} %get-tuple-element.5, s32[]{:T(128)} %constant.41.clone.1), kind=kCustom, calls=%fused_computation.64 | custom fusion | bytes 4100 | tf_op jit(solution)/shard_map/scatter | solution.py:23
  13.6 11.7 %all_to_all.19 = s32[4,1,256]{2,1,0:T(1,128)S(1)} all-to-all(s32[4,1,256]{2,1,0:T(1,128)S(1)} %bitcast.69), channel_id=1, replica_groups=mesh['cfg'=2,'expert'=4,'ffn'=4] {'expert'}, dimensions={0} | all-to-all | bytes 8192 | tf_op jit(solution)/shard_map/all_to_all | solution.py:24
  25.3 5.0 %gather_fusion = bf16[1024,512]{1,0:T(8,128)(2,1)S(1)} fusion(bf16[256,512]{1,0:T(8,128)(2,1)} %param.7, s32[1024]{0:T(1024)S(1)} %broadcast_clamp_fusion), kind=kCustom, calls=%fused_computation | custom fusion | bytes 2101248 | tf_op jit(solution)/shard_map/jit(_take)/gather | solution.py:33
  30.3 1.3 select_select_fusion
  31.6 3.5 %all-to-all-start.1 = ((bf16[4,256,512]{2,1,0:T(8,128)(2,1)}), bf16[4,256,512]{2,1,0:T(8,128)(2,1)S(1)}, u32[]{:S(2)}, u32[]{:S(2)}) async-start(bf16[4,256,512]{2,1,0:T(8,128)(2,1)} %select_select_fusion), calls=%async_computation.1 | async-start | bytes 2097152 | tf_op jit(solution)/shard_map/all_to_all | solution.py:35
  35.1 0.0 all-gather.2.cloned.1.call-start
  35.2 24.5 %all-to-all-done.1 = bf16[4,256,512]{2,1,0:T(8,128)(2,1)S(1)} async-done(((bf16[4,256,512]{2,1,0:T(8,128)(2,1)}), bf16[4,256,512]{2,1,0:T(8,128)(2,1)S(1)}, u32[]{:S(2)}, u32[]{:S(2)}) %all-to-all-start.1) | async-done | bytes 1048608 | tf_op jit(solution)/shard_map/all_to_all | solution.py:35
  59.6 2.0 %gather_fusion.1 = bf16[512,512]{1,0:T(8,128)(2,1)S(1)} fusion(bf16[1024,512]{1,0:T(8,128)(2,1)S(1)} %bitcast.61, s32[1024]{0:T(1024)S(1)} %pad_clamp_fusion), kind=kCustom, calls=%fused_computation.1 | custom fusion | bytes 1050624 | tf_op jit(solution)/shard_map/jit(_take)/gather | solution.py:42
  61.6 0.9 broadcast_select_fusion
  62.5 0.0 all-gather.2.cloned.1.call-update
  62.6 0.0 reduce-scatter.2.cloned.1.call-start
  62.6 21.8 %all-gather.2.cloned.1.call-done = bf16[512,2048]{1,0:T(8,128)(2,1)} async-done(((bf16[512,512]{1,0:T(8,128)(2,1)}), bf16[512,2048]{1,0:T(8,128)(2,1)}) %all-gather.2.cloned.1.call-update) | async-done | bytes 2097168 | tf_op jit(solution)/shard_map/all_gather | solution.py:43
  84.4 0.0 copy-start.2
  84.4 3.5 %fusion.4 = f32[512,256]{1,0:T(8,128)} fusion(bf16[512,2048]{1,0:T(8,128)(2,1)} %all-gather.2.cloned.1.call-done, bf16[1,2048,256]{2,1,0:T(8,128)(2,1)} %param.11), kind=kOutput, calls=%fused_computation.10 | convolution fusion | flops 536870912 | bytes 3670016 | tf_op jit(solution)/shard_map/dot_general | solution.py:44
  87.9 0.0 copy-done
  87.9 0.0 copy-done.2
  87.9 5.0 %convolution_convert_fusion = bf16[512,2048]{1,0:T(8,128)(2,1)} fusion(bf16[512,2048]{1,0:T(8,128)(2,1)S(1)} %copy-done.2, bf16[1,256,2048]{2,1,0:T(8,128)(2,1)S(1)} %copy-done, bf16[1,2048,256]{2,1,0:T(8,128)(2,1)} %param.12, f32[512,256]{1,0:T(8,128)} %fusion.4), kind=kOutput, calls=%fused_computation.4 | convolution fusion | flops 1075576832 | bytes 6815744 | tf_op jit(solution)/shard_map/dot_general | solution.py:47
  92.9 0.0 copy-start.1
  92.9 0.0 reduce-scatter.2.cloned.1.call-update
  93.0 0.7 copy-done.1
  93.6 30.7 %reduce-scatter.2.cloned.1.call-done = bf16[512,512]{1,0:T(8,128)(2,1)} async-done(((bf16[512,2048]{1,0:T(8,128)(2,1)}), bf16[512,512]{1,0:T(8,128)(2,1)}) %reduce-scatter.2.cloned.1.call-update) | async-done | bytes 524304 | tf_op jit(solution)/shard_map/reduce_scatter | solution.py:48
  124.3 3.3 %scatter_custom_fusion.1 = bf16[1024,512]{1,0:T(8,128)(2,1)S(1)} fusion(s32[512]{0:T(512)S(1)} %bitcast.73, bf16[512,512]{1,0:T(8,128)(2,1)} %reduce-scatter.2.cloned.1.call-done, f32[512]{0:T(512)S(1)} %fusion.22, bf16[]{:T(256)} %constant.60.clone.1), kind=kCustom, calls=%fused_computation.15 | custom fusion | flops 786432 | bytes 1574914 | tf_op jit(solution)/shard_map/scatter | solution.py:55
  127.6 30.0 %all_to_all.20 = bf16[4,256,512]{2,1,0:T(8,128)(2,1)S(1)} all-to-all(bf16[4,256,512]{2,1,0:T(8,128)(2,1)S(1)} %bitcast.63), channel_id=1, replica_groups=mesh['cfg'=2,'expert'=4,'ffn'=4] {'expert'}, dimensions={0} | all-to-all | bytes 2097152 | tf_op jit(solution)/shard_map/all_to_all | solution.py:57
  157.5 1.1 convolution_convert_fusion.1
  (9 shorter events, 0.1 us)
Async XLA Ops:
  6.5 81.4 %copy-start = (bf16[1,256,2048]{2,1,0:T(8,128)(2,1)S(1)}, bf16[1,256,2048]{2,1,0:T(8,128)(2,1)}, u32[]{:S(2)}) copy-start(bf16[1,256,2048]{2,1,0:T(8,128)(2,1)} %param.13) | copy-start | bytes 3145732
  31.6 28.1 %all-to-all-start.1 = ((bf16[4,256,512]{2,1,0:T(8,128)(2,1)}), bf16[4,256,512]{2,1,0:T(8,128)(2,1)S(1)}, u32[]{:S(2)}, u32[]{:S(2)}) async-start(bf16[4,256,512]{2,1,0:T(8,128)(2,1)} %select_select_fusion), calls=%async_computation.1 | async-start | bytes 2097152 | tf_op jit(solution)/shard_map/all_to_all | solution.py:35
  35.1 49.3 %all-gather.2.cloned.1.call-start = ((), (), s32[]{:S(2)}) async-start(), calls=%async_computation.4 | async-start | bytes 2621440 | tf_op jit(solution)/shard_map/all_gather | solution.py:43
  62.6 61.7 %reduce-scatter.2.cloned.1.call-start = ((), (), s32[]{:S(2)}) async-start(), calls=%async_computation.5 | async-start | bytes 2621440 | tf_op jit(solution)/shard_map/reduce_scatter | solution.py:48
  84.4 3.5 %copy-start.2 = (bf16[512,2048]{1,0:T(8,128)(2,1)S(1)}, bf16[512,2048]{1,0:T(8,128)(2,1)}, u32[]{:S(2)}) copy-start(bf16[512,2048]{1,0:T(8,128)(2,1)} %all-gather.2.cloned.1.call-done) | copy-start | bytes 6291460
  92.9 0.7 copy-start.1
Sparse Core Ops, SparseCore 0:
  62.7 21.6 all-gather.1
  93.1 31.1 reduce-scatter.1
where the time goes:
time: 166 us
  waiting for transfers between devices  76.9 us (46%)
  blocking collectives  41.7 us (25%)
  between operations  14.2 us (9%)
  local copies, waits for them, and re-layouts  10.3 us (6%)
  matrix products  9.68 us (6%)
  other arithmetic  9.12 us (5%)
  starting transfers between devices  3.6 us (2%)
    reduce_scatter x1, waiting for transfers between devices, shards(): lax.psum_scatter(partial_value.astype(jnp.bfloat16), 'ffn', scatter_dimen...  30.7 us
    all_to_all x1, blocking collectives, shards(): lax.all_to_all(returned_slots.reshape(experts_n, slot_depth, -1), 'expert...  30 us
    all_to_all x1, waiting for transfers between devices, shards(): lax.all_to_all(row_block.reshape(experts_n, slot_depth, -1), 'expert', sp...  24.5 us
    all_gather x1, waiting for transfers between devices, shards(): portion = lax.all_gather(picked, 'ffn', axis=1, tiled=True)  21.8 us
    all_to_all x1, blocking collectives, shards(): lax.all_to_all(request.reshape(experts_n, slot_depth), 'expert', split_ax...  11.7 us
    dot_general x1, matrix products, shards(): jnp.dot(hidden, down_rows, preferred_element_type=jnp.float32)  5.02 us
    gather x1, local copies, waits for them, and re-layouts, shards(): jnp.take(tokens, safe_idx, axis=0)  4.98 us
    dot_general x1, matrix products, shards(): gate_next = jnp.dot(portion, gate_cols, preferred_element_type=jnp.float32)  3.52 us
  transfers between devices with their start and end apart: 3, of which 3 were waited for; matrix products, arithmetic and copies ran while one was open for 0% of the time, Pallas kernels for 0%

commit v1 on v0

--- a/solution.py
+++ b/solution.py
@@ -1,10 +1,14 @@
+import functools
+
 import jax
 import jax.numpy as jnp
 from jax import lax
+from jax.experimental import pallas as pl
+from jax.experimental.pallas import tpu as pltpu
 from jax.sharding import PartitionSpec as P
 
 
-def shards(tokens, chosen, gates, capacity, w_gate, w_up, w_down):
+def shards_general(tokens, chosen, gates, capacity, w_gate, w_up, w_down):
     experts_n = lax.axis_size("expert")
     tok_dev = tokens.shape[0]
     picked_ids = chosen[0]
@@ -69,6 +73,239 @@
     return mixed.astype(jnp.bfloat16)
 
 
+LANES = 128
+KINDS = 13
+MESH = pl.DeviceIdType.MESH
+(TO_RIGHT, TO_LEFT, ON_RIGHT, ON_LEFT, ROWS_X, ROWS_CORE, ROWS_ON,
+ PART_CORE, PART_X, HALF_RIGHT, HALF_LEFT, SUM_RIGHT, SUM_LEFT) = range(KINDS)
+
+
+def dot(a, b):
+    return jnp.dot(a, b, preferred_element_type=jnp.float32)
+
+
+def fused(ring, cap_ref, chosen_ref, gates_ref, tok_ref, wg_ref, wu_ref, wd_ref, out_ref,
+          near, pick, put, live, rows, w_in, w_out, acc, hid, part_out, part_in, own_sum,
+          sum_out, sum_in, far_out, half_in, edge_out, edge_in, own_out,
+          send_sem, recv_sem, load_sem):
+    block, width = tok_ref.shape
+    listed = chosen_ref.shape[1]
+    half = block // 2
+    chunks = width // LANES
+    z = lax.axis_index("expert")
+    f = lax.axis_index("ffn")
+    right = {"expert": lax.rem(z + 1, ring)}
+    left = {"expert": lax.rem(z + ring - 1, ring)}
+    chip, core = f // 2, f % 2
+    slot_id = (f, chip * 2 + 1 - core, (1 - chip) * 2 + core, (1 - chip) * 2 + 1 - core)
+    mate = {"ffn": slot_id[1]}
+    across = {"ffn": slot_id[2]}
+
+    loads = []
+    ff = wg_ref.shape[1]
+    for s in range(4):
+        at = pl.ds(pl.multiple_of(slot_id[s] * width, width), width)
+        loads.append([
+            pltpu.make_async_copy(wg_ref.at[at, :], w_in.at[s, :, 0:ff], load_sem.at[3 * s]),
+            pltpu.make_async_copy(wu_ref.at[at, :], w_in.at[s, :, ff:2 * ff], load_sem.at[3 * s + 1]),
+            pltpu.make_async_copy(wd_ref.at[:, at], w_out.at[s], load_sem.at[3 * s + 2]),
+        ])
+    for group in loads:
+        for load in group:
+            load.start()
+
+    barrier = pltpu.get_barrier_semaphore()
+    for other in (left, right, mate, across):
+        pl.semaphore_signal(barrier, inc=1, device_id=other, device_id_type=MESH)
+    pl.semaphore_wait(barrier, 4)
+
+    def cols(q):
+        return slice(q * LANES, (q + 1) * LANES)
+
+    def copy(kind, q):
+        src, dst, to = {
+            TO_RIGHT: lambda: (tok_ref.at[:, cols(q)], near.at[q, 0:block], right),
+            TO_LEFT: lambda: (tok_ref.at[:, cols(q)], near.at[q, 2 * block:3 * block], left),
+            ON_RIGHT: lambda: (near.at[q, 0:half], near.at[q, block:block + half], right),
+            ON_LEFT: lambda: (near.at[q, 2 * block + half:3 * block], near.at[q, block + half:2 * block], left),
+            ROWS_X: lambda: (rows.at[0, q], rows.at[2, q], across),
+            ROWS_CORE: lambda: (rows.at[0, q], rows.at[1, q], mate),
+            ROWS_ON: lambda: (rows.at[2, q], rows.at[3, q], mate),
+            PART_CORE: lambda: (part_out.at[q], part_in.at[q], mate),
+            PART_X: lambda: (sum_out.at[q], sum_in.at[q], across),
+            HALF_RIGHT: lambda: (far_out.at[q, 0:half], half_in.at[q, 0:half], right),
+            HALF_LEFT: lambda: (far_out.at[q, half:block], half_in.at[q, half:block], left),
+            SUM_RIGHT: lambda: (edge_out.at[q, 0], edge_in.at[q, 0], right),
+            SUM_LEFT: lambda: (edge_out.at[q, 1], edge_in.at[q, 1], left),
+        }[kind]()
+        i = kind * chunks + q
+        return pltpu.make_async_remote_copy(
+            src_ref=src, dst_ref=dst, send_sem=send_sem.at[i], recv_sem=recv_sem.at[i],
+            device_id=to, device_id_type=MESH)
+
+    def start(kind, q):
+        copy(kind, q).start()
+
+    def got(kind, q):
+        copy(kind, q).wait_recv()
+
+    def own(q):
+        start(TO_RIGHT, q)
+        start(TO_LEFT, q)
+
+    own(0)
+    own(1)
+
+    ids = chosen_ref[...]
+    ids_col = jnp.broadcast_to(ids.astype(jnp.float32), (LANES, listed)).T.astype(jnp.int32)
+    lane = lax.broadcasted_iota(jnp.int32, (listed, LANES), 1)
+    for r in range(4):
+        base = lax.rem(z + ring - r, ring) * block
+        for h in range(block // LANES):
+            hit = ids_col == lane + (base + h * LANES)
+            pick[:, r * block + h * LANES:r * block + (h + 1) * LANES] = jnp.where(hit, 1.0, 0.0).astype(jnp.bfloat16)
+
+    def select(q):
+        got(ON_RIGHT, q)
+        got(ON_LEFT, q)
+        chosen_rows = dot(pick[:, 0:block], tok_ref[:, cols(q)]) + dot(pick[:, block:], near[q])
+        rows[0, q] = chosen_rows.astype(jnp.bfloat16)
+        start(ROWS_X, q)
+        start(ROWS_CORE, q)
+
+    for q in range(chunks):
+        got(TO_RIGHT, q)
+        start(ON_RIGHT, q)
+        got(TO_LEFT, q)
+        start(ON_LEFT, q)
+        if q + 2 < chunks:
+            own(q + 2)
+        if q >= 1:
+            select(q - 1)
+    select(chunks - 1)
+
+    token = lax.broadcasted_iota(jnp.int32, (block, listed), 0)
+    for r in range(4):
+        base = lax.rem(z + ring - r, ring) * block
+        put[r] = jnp.where(ids == token + base, 1.0, 0.0).astype(jnp.bfloat16)
+    position = lax.broadcasted_iota(jnp.int32, (1, listed), 1)
+    kept = jnp.where(position < cap_ref[0], gates_ref[...], 0.0)
+    live[...] = jnp.broadcast_to(kept, (LANES, listed)).T
+
+    for group in loads:
+        for load in group:
+            load.wait()
+
+    def whole(s):
+        return jnp.concatenate([rows[s, q] for q in range(chunks)], axis=1)
+
+    acc[...] = dot(whole(0), w_in[0])
+    for q in range(chunks):
+        got(ROWS_CORE, q)
+    acc[...] += dot(whole(1), w_in[1])
+
+    def add(s, q):
+        acc[...] += dot(rows[s, q], w_in[s, q * LANES:(q + 1) * LANES])
+
+    for q in range(chunks):
+        got(ROWS_X, q)
+        start(ROWS_ON, q)
+        add(2, q)
+        if q >= 1:
+            got(ROWS_ON, q - 1)
+            add(3, q - 1)
+    got(ROWS_ON, chunks - 1)
+    add(3, chunks - 1)
+
+    gate = acc[:, 0:ff]
+    hid[...] = (gate / (1.0 + jnp.exp(-gate)) * acc[:, ff:2 * ff]).astype(jnp.bfloat16)
+
+    for q in range(chunks):
+        both = jnp.concatenate([w_out[1, :, cols(q)], w_out[3, :, cols(q)]], axis=1)
+        part_out[q] = dot(hid[...], both).astype(jnp.bfloat16)
+        start(PART_CORE, q)
+    for q in range(chunks):
+        both = dot(hid[...], jnp.concatenate([w_out[0, :, cols(q)], w_out[2, :, cols(q)]], axis=1))
+        got(PART_CORE, q)
+        both = both + part_in[q].astype(jnp.float32)
+        sum_out[q] = both[:, LANES:].astype(jnp.bfloat16)
+        start(PART_X, q)
+        own_sum[q] = both[:, :LANES]
+
+    def finish(q):
+        got(SUM_RIGHT, q)
+        got(SUM_LEFT, q)
+        total = own_out[q] + edge_in[q, 0].astype(jnp.float32) + edge_in[q, 1].astype(jnp.float32)
+        out_ref[:, cols(q)] = total.astype(jnp.bfloat16)
+
+    for q in range(chunks):
+        got(PART_X, q)
+        y = own_sum[q] + sum_in[q].astype(jnp.float32)
+        weighted = (live[...] * y).astype(jnp.bfloat16)
+        far_out[q] = dot(put[2], weighted).astype(jnp.bfloat16)
+        start(HALF_RIGHT, q)
+        start(HALF_LEFT, q)
+        to_right = dot(put[3], weighted)
+        to_left = dot(put[1], weighted)
+        own_out[q] = dot(put[0], weighted)
+        if q >= 1:
+            finish(q - 1)
+        got(HALF_RIGHT, q)
+        edge_out[q, 0, 0:half] = (to_right[0:half] + half_in[q, 0:half].astype(jnp.float32)).astype(jnp.bfloat16)
+        edge_out[q, 0, half:block] = to_right[half:block].astype(jnp.bfloat16)
+        start(SUM_RIGHT, q)
+        got(HALF_LEFT, q)
+        edge_out[q, 1, half:block] = (to_left[half:block] + half_in[q, half:block].astype(jnp.float32)).astype(jnp.bfloat16)
+        edge_out[q, 1, 0:half] = to_left[0:half].astype(jnp.bfloat16)
+        start(SUM_LEFT, q)
+    finish(chunks - 1)
+
+    for kind in range(KINDS):
+        for q in range(chunks):
+            copy(kind, q).wait_send()
+
+
+def shards_fused(ring, tokens, chosen, gates, capacity, w_gate, w_up, w_down):
+    block, width = tokens.shape
+    listed = chosen.shape[1]
+    ff = w_gate.shape[2]
+    chunks = width // LANES
+    bf16, f32 = jnp.bfloat16, jnp.float32
+    vmem = pl.BlockSpec(memory_space=pltpu.VMEM)
+    far = pl.BlockSpec(memory_space=pl.ANY)
+    return pl.pallas_call(
+        functools.partial(fused, ring),
+        out_shape=jax.ShapeDtypeStruct(tokens.shape, bf16),
+        in_specs=[pl.BlockSpec(memory_space=pltpu.SMEM), vmem, vmem, vmem, far, far, far],
+        out_specs=vmem,
+        scratch_shapes=[
+            pltpu.VMEM((chunks, 3 * block, LANES), bf16),
+            pltpu.VMEM((listed, 4 * block), bf16),
+            pltpu.VMEM((4, block, listed), bf16),
+            pltpu.VMEM((listed, LANES), f32),
+            pltpu.VMEM((4, chunks, listed, LANES), bf16),
+            pltpu.VMEM((4, width, 2 * ff), bf16),
+            pltpu.VMEM((4, ff, width), bf16),
+            pltpu.VMEM((listed, 2 * ff), f32),
+            pltpu.VMEM((listed, ff), bf16),
+            pltpu.VMEM((chunks, listed, 2 * LANES), bf16),
+            pltpu.VMEM((chunks, listed, 2 * LANES), bf16),
+            pltpu.VMEM((chunks, listed, LANES), f32),
+            pltpu.VMEM((chunks, listed, LANES), bf16),
+            pltpu.VMEM((chunks, listed, LANES), bf16),
+            pltpu.VMEM((chunks, block, LANES), bf16),
+            pltpu.VMEM((chunks, block, LANES), bf16),
+            pltpu.VMEM((chunks, 2, block, LANES), bf16),
+            pltpu.VMEM((chunks, 2, block, LANES), bf16),
+            pltpu.VMEM((chunks, block, LANES), f32),
+            pltpu.SemaphoreType.DMA((KINDS * chunks,)),
+            pltpu.SemaphoreType.DMA((KINDS * chunks,)),
+            pltpu.SemaphoreType.DMA((12,)),
+        ],
+        compiler_params=pltpu.CompilerParams(collective_id=0, has_side_effects=True),
+    )(capacity, chosen, gates, tokens, w_gate[0], w_up[0], w_down[0])
+
+
 def solution(mesh):
     in_specs = (
         P(("cfg", "expert"), "ffn"),
@@ -80,4 +317,7 @@
         P("expert", "ffn", None),
     )
     out_specs = P(("cfg", "expert"), "ffn")
-    return jax.shard_map(shards, mesh=mesh, in_specs=in_specs, out_specs=out_specs, check_vma=False)
+    ring = mesh.shape["expert"]
+    small = ring == 4 and mesh.shape["ffn"] == 4
+    body = functools.partial(shards_fused, ring) if small else shards_general
+    return jax.shard_map(body, mesh=mesh, in_specs=in_specs, out_specs=out_specs, check_vma=False)

time: 166 us -> 70.7 us (0.43)
  waiting for transfers between devices: 76.9 us -> 0 us
  Pallas kernels: 0 us -> 68.2 us
  blocking collectives: 41.7 us -> 0 us
  between operations: 14.2 us -> 0.66 us
  matrix products: 9.68 us -> 0 us
  other arithmetic: 9.12 us -> 0 us
  local copies, waits for them, and re-layouts: 10.3 us -> 1.67 us
  starting transfers between devices: 3.6 us -> 0 us
    pallas_call x0 -> x1, Pallas kernels: none -> 68.2 us  [shards_fused(): pl.pallas_call(functools.partial(fused, ring), out_shape=jax.ShapeDtypeSt...]
    all_to_all x2 -> x0, blocking collectives: 41.7 us -> none  [the longest x1 30 us: shards(): lax.all_to_all(returned_slots.reshape(experts_n, slot_depth, -1), 'expert...]
    reduce_scatter x1 -> x0, waiting for transfers between devices: 30.7 us -> none  [shards(): lax.psum_scatter(partial_value.astype(jnp.bfloat16), 'ffn', scatter_dimen...]
    all_to_all x1 -> x0, waiting for transfers between devices: 24.5 us -> none  [shards(): lax.all_to_all(row_block.reshape(experts_n, slot_depth, -1), 'expert', sp...]
    all_gather x1 -> x0, waiting for transfers between devices: 21.8 us -> none  [shards(): portion = lax.all_gather(picked, 'ffn', axis=1, tiled=True)]
    dot_general x3 -> x0, matrix products: 9.68 us -> none  [the longest x1 5.02 us: shards(): jnp.dot(hidden, down_rows, preferred_element_type=jnp.float32)]
    gather x2 -> x0, local copies, waits for them, and re-layouts: 6.94 us -> none  [the longest x1 4.98 us: shards(): jnp.take(tokens, safe_idx, axis=0)]
    select_n x6 -> x0, other arithmetic: 4.29 us -> none  [the longest x1 1.26 us: shards(): jnp.where(usable[:, None], jnp.take(tokens, safe_idx, axis=0), jnp.zeros(...]
  transfers between devices with their start and end apart: 3 -> 0, of which waited for: 3 -> 0; matrix products, arithmetic and copies ran while one was open for 0% -> 0% of each run, Pallas kernels for 0% -> 0%
where the time goes in v1:
time: 70.7 us; the launch traced here: 70.5 us
  Pallas kernels  68.2 us (96%)
  local copies, waits for them, and re-layouts  1.67 us (2%)
    pallas_call x1, Pallas kernels, shards_fused(): pl.pallas_call(functools.partial(fused, ring), out_shape=jax.ShapeDtypeSt...  68.2 us
    unnamed x1, local copies, waits for them, and re-layouts  1.67 us

profile of v1, /device:TPU:0, one launch (start us, length us, event | category | flops | bytes accessed | tf_op | source)
XLA Modules:
  0.0 70.5 jit_solution(10331626841860378958)
XLA Ops:
  0.7 68.2 %shard_map.73 = bf16[256,512]{1,0:T(8,128)(2,1)} custom-call(s32[1]{0:T(128)S(6)} %copy.9.cap_ref, s32[1,512]{1,0:T(1,128)} %chosen_ref.1, f32[1,512]{1,0:T(1,128)} %gates_ref.1, bf16[256,512]{1,0:T(8,128)(2,1)} %tok_ref.1, bf16[2048,256]{1,0:T(8,128)(2,1)} %bitcast.3, bf16[2048,256]{1,0:T(8,128)(2,1)} %bitcast.4, bf16[256,2048]{1,0:T(8,128)(2,1)} %bitcast.5), custom_call_target="tpu_custom_call" | custom-call | tf_op jit(solution)/shard_map/pallas_call | solution.py:276
  68.8 1.7 %copy.10 = bf16[256,512]{1,0:T(8,128)(2,1)} copy(bf16[256,512]{1,0:T(8,128)(2,1)} %shard_map.73) | data formatting | bytes 524288

commit v2 on v1

--- a/solution.py
+++ b/solution.py
@@ -86,7 +86,7 @@
 
 def fused(ring, cap_ref, chosen_ref, gates_ref, tok_ref, wg_ref, wu_ref, wd_ref, out_ref,
           near, pick, put, live, rows, w_in, w_out, acc, hid, part_out, part_in, own_sum,
-          sum_out, sum_in, far_out, half_in, edge_out, edge_in, own_out,
+          sum_out, sum_in, far_out, half_in, edges, edge_out, edge_in, own_out,
           send_sem, recv_sem, load_sem):
     block, width = tok_ref.shape
     listed = chosen_ref.shape[1]
@@ -153,8 +153,8 @@
         start(TO_RIGHT, q)
         start(TO_LEFT, q)
 
-    own(0)
-    own(1)
+    for q in range(min(3, chunks)):
+        own(q)
 
     ids = chosen_ref[...]
     ids_col = jnp.broadcast_to(ids.astype(jnp.float32), (LANES, listed)).T.astype(jnp.int32)
@@ -178,8 +178,8 @@
         start(ON_RIGHT, q)
         got(TO_LEFT, q)
         start(ON_LEFT, q)
-        if q + 2 < chunks:
-            own(q + 2)
+        if q + 3 < chunks:
+            own(q + 3)
         if q >= 1:
             select(q - 1)
     select(chunks - 1)
@@ -238,27 +238,34 @@
         total = own_out[q] + edge_in[q, 0].astype(jnp.float32) + edge_in[q, 1].astype(jnp.float32)
         out_ref[:, cols(q)] = total.astype(jnp.bfloat16)
 
-    for q in range(chunks):
+    def spread(q):
         got(PART_X, q)
         y = own_sum[q] + sum_in[q].astype(jnp.float32)
         weighted = (live[...] * y).astype(jnp.bfloat16)
         far_out[q] = dot(put[2], weighted).astype(jnp.bfloat16)
         start(HALF_RIGHT, q)
         start(HALF_LEFT, q)
-        to_right = dot(put[3], weighted)
-        to_left = dot(put[1], weighted)
+        edges[q, 0] = dot(put[3], weighted)
+        edges[q, 1] = dot(put[1], weighted)
         own_out[q] = dot(put[0], weighted)
-        if q >= 1:
-            finish(q - 1)
+
+    def merge(q):
         got(HALF_RIGHT, q)
-        edge_out[q, 0, 0:half] = (to_right[0:half] + half_in[q, 0:half].astype(jnp.float32)).astype(jnp.bfloat16)
-        edge_out[q, 0, half:block] = to_right[half:block].astype(jnp.bfloat16)
+        edge_out[q, 0, 0:half] = (edges[q, 0, 0:half] + half_in[q, 0:half].astype(jnp.float32)).astype(jnp.bfloat16)
+        edge_out[q, 0, half:block] = edges[q, 0, half:block].astype(jnp.bfloat16)
         start(SUM_RIGHT, q)
         got(HALF_LEFT, q)
-        edge_out[q, 1, half:block] = (to_left[half:block] + half_in[q, half:block].astype(jnp.float32)).astype(jnp.bfloat16)
-        edge_out[q, 1, 0:half] = to_left[0:half].astype(jnp.bfloat16)
+        edge_out[q, 1, half:block] = (edges[q, 1, half:block] + half_in[q, half:block].astype(jnp.float32)).astype(jnp.bfloat16)
+        edge_out[q, 1, 0:half] = edges[q, 1, 0:half].astype(jnp.bfloat16)
         start(SUM_LEFT, q)
-    finish(chunks - 1)
+
+    for q in range(chunks + 2):
+        if q < chunks:
+            spread(q)
+        if 1 <= q <= chunks:
+            merge(q - 1)
+        if q >= 2:
+            finish(q - 2)
 
     for kind in range(KINDS):
         for q in range(chunks):
@@ -295,6 +302,7 @@
             pltpu.VMEM((chunks, listed, LANES), bf16),
             pltpu.VMEM((chunks, block, LANES), bf16),
             pltpu.VMEM((chunks, block, LANES), bf16),
+            pltpu.VMEM((chunks, 2, block, LANES), f32),
             pltpu.VMEM((chunks, 2, block, LANES), bf16),
             pltpu.VMEM((chunks, 2, block, LANES), bf16),
             pltpu.VMEM((chunks, block, LANES), f32),

time: 70.7 us -> 64.7 us (0.915)
  Pallas kernels: 68.2 us -> 62.2 us
    pallas_call x1, Pallas kernels: 68.2 us -> 62.2 us  [shards_fused(): pl.pallas_call(functools.partial(fused, ring), out_shape=jax.ShapeDtypeSt...]
where the time goes in v2:
time: 64.7 us; the launch traced here: 64.5 us
  Pallas kernels  62.2 us (96%)
  local copies, waits for them, and re-layouts  1.67 us (3%)
  between operations  0.66 us (1%)
    pallas_call x1, Pallas kernels, shards_fused(): pl.pallas_call(functools.partial(fused, ring), out_shape=jax.ShapeDtypeSt...  62.2 us
    unnamed x1, local copies, waits for them, and re-layouts  1.67 us

profile of v2, /device:TPU:0, one launch (start us, length us, event | category | flops | bytes accessed | tf_op | source)
XLA Modules:
  0.0 64.5 jit_solution(11662410592739622724)
XLA Ops:
  0.7 62.2 %shard_map.73 = bf16[256,512]{1,0:T(8,128)(2,1)} custom-call(s32[1]{0:T(128)S(6)} %copy.9.cap_ref, s32[1,512]{1,0:T(1,128)} %chosen_ref.1, f32[1,512]{1,0:T(1,128)} %gates_ref.1, bf16[256,512]{1,0:T(8,128)(2,1)} %tok_ref.1, bf16[2048,256]{1,0:T(8,128)(2,1)} %bitcast.3, bf16[2048,256]{1,0:T(8,128)(2,1)} %bitcast.4, bf16[256,2048]{1,0:T(8,128)(2,1)} %bitcast.5), custom_call_target="tpu_custom_call" | custom-call | tf_op jit(solution)/shard_map/pallas_call | solution.py:283
  62.8 1.7 %copy.10 = bf16[256,512]{1,0:T(8,128)(2,1)} copy(bf16[256,512]{1,0:T(8,128)(2,1)} %shard_map.73) | data formatting | bytes 524288

commit v3 on v2

--- a/solution.py
+++ b/solution.py
@@ -87,7 +87,7 @@
 def fused(ring, cap_ref, chosen_ref, gates_ref, tok_ref, wg_ref, wu_ref, wd_ref, out_ref,
           near, pick, put, live, rows, w_in, w_out, acc, hid, part_out, part_in, own_sum,
           sum_out, sum_in, far_out, half_in, edges, edge_out, edge_in, own_out,
-          send_sem, recv_sem, load_sem):
+          send_sem, recv_sem, load_sem, mate_in):
     block, width = tok_ref.shape
     listed = chosen_ref.shape[1]
     half = block // 2
@@ -115,9 +115,21 @@
             load.start()
 
     barrier = pltpu.get_barrier_semaphore()
-    for other in (left, right, mate, across):
+    for other in (left, right, across):
         pl.semaphore_signal(barrier, inc=1, device_id=other, device_id_type=MESH)
-    pl.semaphore_wait(barrier, 4)
+
+    @pl.when(core == 0)
+    def _():
+        pl.semaphore_signal(barrier, inc=1, device_id=mate, device_id_type=MESH)
+
+    @pl.when(core == 0)
+    def _():
+        pl.semaphore_wait(barrier, 3)
+
+    @pl.when(core == 1)
+    def _():
+        pl.semaphore_wait(barrier, 4)
+        pl.semaphore_signal(mate_in, inc=1, device_id=mate, device_id_type=MESH)
 
     def cols(q):
         return slice(q * LANES, (q + 1) * LANES)
@@ -153,17 +165,19 @@
         start(TO_RIGHT, q)
         start(TO_LEFT, q)
 
-    for q in range(min(3, chunks)):
+    for q in range(min(2, chunks)):
         own(q)
 
     ids = chosen_ref[...]
-    ids_col = jnp.broadcast_to(ids.astype(jnp.float32), (LANES, listed)).T.astype(jnp.int32)
-    lane = lax.broadcasted_iota(jnp.int32, (listed, LANES), 1)
-    for r in range(4):
-        base = lax.rem(z + ring - r, ring) * block
-        for h in range(block // LANES):
-            hit = ids_col == lane + (base + h * LANES)
-            pick[:, r * block + h * LANES:r * block + (h + 1) * LANES] = jnp.where(hit, 1.0, 0.0).astype(jnp.bfloat16)
+
+    def mark():
+        ids_col = jnp.broadcast_to(ids.astype(jnp.float32), (LANES, listed)).T.astype(jnp.int32)
+        lane = lax.broadcasted_iota(jnp.int32, (listed, LANES), 1)
+        for r in range(4):
+            base = lax.rem(z + ring - r, ring) * block
+            for h in range(block // LANES):
+                hit = ids_col == lane + (base + h * LANES)
+                pick[:, r * block + h * LANES:r * block + (h + 1) * LANES] = jnp.where(hit, 1.0, 0.0).astype(jnp.bfloat16)
 
     def select(q):
         got(ON_RIGHT, q)
@@ -171,18 +185,26 @@
         chosen_rows = dot(pick[:, 0:block], tok_ref[:, cols(q)]) + dot(pick[:, block:], near[q])
         rows[0, q] = chosen_rows.astype(jnp.bfloat16)
         start(ROWS_X, q)
-        start(ROWS_CORE, q)
 
     for q in range(chunks):
         got(TO_RIGHT, q)
         start(ON_RIGHT, q)
         got(TO_LEFT, q)
         start(ON_LEFT, q)
-        if q + 3 < chunks:
-            own(q + 3)
-        if q >= 1:
+        if q + 2 < chunks:
+            own(q + 2)
+        if q == 0:
+            mark()
+        else:
             select(q - 1)
     select(chunks - 1)
+
+    @pl.when(core == 0)
+    def _():
+        pl.semaphore_wait(mate_in, 1)
+
+    for q in range(chunks):
+        start(ROWS_CORE, q)
 
     token = lax.broadcasted_iota(jnp.int32, (block, listed), 0)
     for r in range(4):
@@ -309,6 +331,7 @@
             pltpu.SemaphoreType.DMA((KINDS * chunks,)),
             pltpu.SemaphoreType.DMA((KINDS * chunks,)),
             pltpu.SemaphoreType.DMA((12,)),
+            pltpu.SemaphoreType.REGULAR,
         ],
         compiler_params=pltpu.CompilerParams(collective_id=0, has_side_effects=True),
     )(capacity, chosen, gates, tokens, w_gate[0], w_up[0], w_down[0])

time: 64.7 us -> 63.3 us (0.978)
  Pallas kernels: 62.2 us -> 60.8 us
    pallas_call x1, Pallas kernels: 62.2 us -> 60.8 us  [shards_fused(): pl.pallas_call(functools.partial(fused, ring), out_shape=jax.ShapeDtypeSt...]
where the time goes in v3:
time: 63.3 us; the launch traced here: 63.1 us
  Pallas kernels  60.8 us (96%)
  local copies, waits for them, and re-layouts  1.67 us (3%)
  between operations  0.66 us (1%)
    pallas_call x1, Pallas kernels, shards_fused(): pl.pallas_call(functools.partial(fused, ring), out_shape=jax.ShapeDtypeSt...  60.8 us
    unnamed x1, local copies, waits for them, and re-layouts  1.67 us

profile of v3, /device:TPU:0, one launch (start us, length us, event | category | flops | bytes accessed | tf_op | source)
XLA Modules:
  0.0 63.1 jit_solution(3675300744719821181)
XLA Ops:
  0.7 60.8 %shard_map.73 = bf16[256,512]{1,0:T(8,128)(2,1)} custom-call(s32[1]{0:T(128)S(6)} %copy.9.cap_ref, s32[1,512]{1,0:T(1,128)} %chosen_ref.1, f32[1,512]{1,0:T(1,128)} %gates_ref.1, bf16[256,512]{1,0:T(8,128)(2,1)} %tok_ref.1, bf16[2048,256]{1,0:T(8,128)(2,1)} %bitcast.3, bf16[2048,256]{1,0:T(8,128)(2,1)} %bitcast.4, bf16[256,2048]{1,0:T(8,128)(2,1)} %bitcast.5), custom_call_target="tpu_custom_call" | custom-call | tf_op jit(solution)/shard_map/pallas_call | solution.py:305
  61.5 1.7 %copy.10 = bf16[256,512]{1,0:T(8,128)(2,1)} copy(bf16[256,512]{1,0:T(8,128)(2,1)} %shard_map.73) | data formatting | bytes 524288

commit v4 on v3

--- a/solution.py
+++ b/solution.py
@@ -74,10 +74,11 @@
 
 
 LANES = 128
-KINDS = 13
+KINDS = 15
 MESH = pl.DeviceIdType.MESH
 (TO_RIGHT, TO_LEFT, ON_RIGHT, ON_LEFT, ROWS_X, ROWS_CORE, ROWS_ON,
- PART_CORE, PART_X, HALF_RIGHT, HALF_LEFT, SUM_RIGHT, SUM_LEFT) = range(KINDS)
+ PART_CORE, PART_X, HALF_RIGHT, HALF_LEFT, SUM_RIGHT, SUM_LEFT,
+ PLAIN_RIGHT, PLAIN_LEFT) = range(KINDS)
 
 
 def dot(a, b):
@@ -94,8 +95,13 @@
     chunks = width // LANES
     z = lax.axis_index("expert")
     f = lax.axis_index("ffn")
-    right = {"expert": lax.rem(z + 1, ring)}
-    left = {"expert": lax.rem(z + ring - 1, ring)}
+
+    def member(p):
+        return p + (p // 2) * (2 * ring - 3 - 2 * p)
+
+    spot = member(z)
+    right = {"expert": member(lax.rem(spot + 1, ring))}
+    left = {"expert": member(lax.rem(spot + ring - 1, ring))}
     chip, core = f // 2, f % 2
     slot_id = (f, chip * 2 + 1 - core, (1 - chip) * 2 + core, (1 - chip) * 2 + 1 - core)
     mate = {"ffn": slot_id[1]}
@@ -147,8 +153,10 @@
             PART_X: lambda: (sum_out.at[q], sum_in.at[q], across),
             HALF_RIGHT: lambda: (far_out.at[q, 0:half], half_in.at[q, 0:half], right),
             HALF_LEFT: lambda: (far_out.at[q, half:block], half_in.at[q, half:block], left),
-            SUM_RIGHT: lambda: (edge_out.at[q, 0], edge_in.at[q, 0], right),
-            SUM_LEFT: lambda: (edge_out.at[q, 1], edge_in.at[q, 1], left),
+            SUM_RIGHT: lambda: (edge_out.at[q, 0, 0:half], edge_in.at[q, 0, 0:half], right),
+            SUM_LEFT: lambda: (edge_out.at[q, 1, half:block], edge_in.at[q, 1, half:block], left),
+            PLAIN_RIGHT: lambda: (edge_out.at[q, 0, half:block], edge_in.at[q, 0, half:block], right),
+            PLAIN_LEFT: lambda: (edge_out.at[q, 1, 0:half], edge_in.at[q, 1, 0:half], left),
         }[kind]()
         i = kind * chunks + q
         return pltpu.make_async_remote_copy(
@@ -174,7 +182,7 @@
         ids_col = jnp.broadcast_to(ids.astype(jnp.float32), (LANES, listed)).T.astype(jnp.int32)
         lane = lax.broadcasted_iota(jnp.int32, (listed, LANES), 1)
         for r in range(4):
-            base = lax.rem(z + ring - r, ring) * block
+            base = member(lax.rem(spot + ring - r, ring)) * block
             for h in range(block // LANES):
                 hit = ids_col == lane + (base + h * LANES)
                 pick[:, r * block + h * LANES:r * block + (h + 1) * LANES] = jnp.where(hit, 1.0, 0.0).astype(jnp.bfloat16)
@@ -208,7 +216,7 @@
 
     token = lax.broadcasted_iota(jnp.int32, (block, listed), 0)
     for r in range(4):
-        base = lax.rem(z + ring - r, ring) * block
+        base = member(lax.rem(spot + ring - r, ring)) * block
         put[r] = jnp.where(ids == token + base, 1.0, 0.0).astype(jnp.bfloat16)
     position = lax.broadcasted_iota(jnp.int32, (1, listed), 1)
     kept = jnp.where(position < cap_ref[0], gates_ref[...], 0.0)
@@ -257,6 +265,8 @@
     def finish(q):
         got(SUM_RIGHT, q)
         got(SUM_LEFT, q)
+        got(PLAIN_RIGHT, q)
+        got(PLAIN_LEFT, q)
         total = own_out[q] + edge_in[q, 0].astype(jnp.float32) + edge_in[q, 1].astype(jnp.float32)
         out_ref[:, cols(q)] = total.astype(jnp.bfloat16)
 
@@ -267,18 +277,22 @@
         far_out[q] = dot(put[2], weighted).astype(jnp.bfloat16)
         start(HALF_RIGHT, q)
         start(HALF_LEFT, q)
-        edges[q, 0] = dot(put[3], weighted)
-        edges[q, 1] = dot(put[1], weighted)
+        to_right = dot(put[3], weighted)
+        to_left = dot(put[1], weighted)
+        edge_out[q, 0, half:block] = to_right[half:block].astype(jnp.bfloat16)
+        edge_out[q, 1, 0:half] = to_left[0:half].astype(jnp.bfloat16)
+        start(PLAIN_RIGHT, q)
+        start(PLAIN_LEFT, q)
+        edges[q, 0] = to_right[0:half]
+        edges[q, 1] = to_left[half:block]
         own_out[q] = dot(put[0], weighted)
 
     def merge(q):
         got(HALF_RIGHT, q)
-        edge_out[q, 0, 0:half] = (edges[q, 0, 0:half] + half_in[q, 0:half].astype(jnp.float32)).astype(jnp.bfloat16)
-        edge_out[q, 0, half:block] = edges[q, 0, half:block].astype(jnp.bfloat16)
+        edge_out[q, 0, 0:half] = (edges[q, 0] + half_in[q, 0:half].astype(jnp.float32)).astype(jnp.bfloat16)
         start(SUM_RIGHT, q)
         got(HALF_LEFT, q)
-        edge_out[q, 1, half:block] = (edges[q, 1, half:block] + half_in[q, half:block].astype(jnp.float32)).astype(jnp.bfloat16)
-        edge_out[q, 1, 0:half] = edges[q, 1, 0:half].astype(jnp.bfloat16)
+        edge_out[q, 1, half:block] = (edges[q, 1] + half_in[q, half:block].astype(jnp.float32)).astype(jnp.bfloat16)
         start(SUM_LEFT, q)
 
     for q in range(chunks + 2):
@@ -324,7 +338,7 @@
             pltpu.VMEM((chunks, listed, LANES), bf16),
             pltpu.VMEM((chunks, block, LANES), bf16),
             pltpu.VMEM((chunks, block, LANES), bf16),
-            pltpu.VMEM((chunks, 2, block, LANES), f32),
+            pltpu.VMEM((chunks, 2, block // 2, LANES), f32),
             pltpu.VMEM((chunks, 2, block, LANES), bf16),
             pltpu.VMEM((chunks, 2, block, LANES), bf16),
             pltpu.VMEM((chunks, block, LANES), f32),

time: 63.3 us -> 62.2 us (0.983)
  Pallas kernels: 60.8 us -> 59.7 us
    pallas_call x1, Pallas kernels: 60.8 us -> 59.7 us  [shards_fused(): pl.pallas_call(functools.partial(fused, ring), out_shape=jax.ShapeDtypeSt...]
where the time goes in v4:
time: 62.2 us; the launch traced here: 62.1 us
  Pallas kernels  59.7 us (96%)
  local copies, waits for them, and re-layouts  1.67 us (3%)
  between operations  0.66 us (1%)
    pallas_call x1, Pallas kernels, shards_fused(): pl.pallas_call(functools.partial(fused, ring), out_shape=jax.ShapeDtypeSt...  59.7 us
    unnamed x1, local copies, waits for them, and re-layouts  1.67 us

profile of v4, /device:TPU:0, one launch (start us, length us, event | category | flops | bytes accessed | tf_op | source)
XLA Modules:
  0.0 62.1 jit_solution(13272272986971277644)
XLA Ops:
  0.7 59.7 %shard_map.73 = bf16[256,512]{1,0:T(8,128)(2,1)} custom-call(s32[1]{0:T(128)S(6)} %copy.9.cap_ref, s32[1,512]{1,0:T(1,128)} %chosen_ref.1, f32[1,512]{1,0:T(1,128)} %gates_ref.1, bf16[256,512]{1,0:T(8,128)(2,1)} %tok_ref.1, bf16[2048,256]{1,0:T(8,128)(2,1)} %bitcast.3, bf16[2048,256]{1,0:T(8,128)(2,1)} %bitcast.4, bf16[256,2048]{1,0:T(8,128)(2,1)} %bitcast.5), custom_call_target="tpu_custom_call" | custom-call | tf_op jit(solution)/shard_map/pallas_call | solution.py:319
  60.4 1.7 %copy.10 = bf16[256,512]{1,0:T(8,128)(2,1)} copy(bf16[256,512]{1,0:T(8,128)(2,1)} %shard_map.73) | data formatting | bytes 524288
